TPU v7x, 128 devices: a 2x2x16 block of a 8x8x16 slice. The times are simulated.
128 devices in a mesh: groups: 4 (over y, x), wide: 32 (over z, core).
Axes of the slice: x: 2, y: 2, z: 16, core: 2. Of those that a mesh axis runs over, the one named last changes fastest.
The devices are a block of a 8x8x16 slice.
Arguments:
- alignment_token_ids: int32 [1024, 512], P(('groups', 'wide')), parts along dimension 0, may hold values from 0 to 22
- residue_index_offsets: int32 [2048], P('groups'), parts along dimension 0, may hold values from 0 to 20480, as said below
- target_residue_feature: float32 [2048, 256], P('groups'), parts along dimension 0, may hold values from -6 to 6
- token_embedding_table: float32 [23, 256], replicated, may hold values from -6 to 6
- attention_norm_gain: float32 [256], replicated, may hold values from 0.1 to 1.9
- query_weight: bfloat16 [256, 256], replicated, may hold values from -1 to 1
- key_weight: bfloat16 [256, 256], replicated, may hold values from -25 to 25
- value_weight: bfloat16 [256, 256], replicated, may hold values from -0.375 to 0.375
- gate_weight: bfloat16 [256, 256], replicated, may hold values from -0.375 to 0.375
- gate_offset_bias: float32 [256], replicated, may hold values from -4 to 4
- output_weight: bfloat16 [256, 256], replicated, may hold values from -0.375 to 0.375
- relative_position_table: float32 [65, 8], replicated, may hold values from -4 to 4
- product_norm_gain: float32 [256], replicated, may hold values from 0.1 to 1.9
- left_weight: bfloat16 [256, 32], replicated, may hold values from -0.375 to 0.375
- right_weight: bfloat16 [256, 32], replicated, may hold values from -0.375 to 0.375
- pair_weight: bfloat16 [1024, 128], replicated, may hold values from -0.375 to 0.375
- pair_projection_bias: float32 [128], replicated, may hold values from -3 to 3
Outputs:
- alignment_updated: float32 [1024, 512, 256], P(('groups', 'wide')), parts along dimension 0
- pair: float32 [2048, 512, 128], P(('groups', 'wide')), parts along dimension 0
There are 4 independent parts, one for each index of `groups`. A program takes and returns all parts, laid end to end along the dimension named above; an argument that names none is the same for every part. Nothing has to cross between parts.
Inputs may be any that keep to these rules, and one draw needn't show every extreme that they name: `residue_index_offsets`: rises by 1 from residue to residue within a chain and by more at chain breaks; the first entry is 0 and the last is 20480.
All inputs are finite; a program needn't handle non-finite values.
Results may differ from a plain program's by a relative error of at most 0.0045.
Values may be sent and summed in bfloat16 or wider, within the bound.
A program may use at most 128 MiB of HBM per device.

v0:
```python
import jax
import jax.numpy as jnp
from jax import lax
from jax.sharding import PartitionSpec as P

REACH = 32


def layer_normalize(values, gain):
    center = jnp.mean(values, axis=-1, keepdims=True)
    centred = values - center
    spread = jnp.mean(centred * centred, axis=-1, keepdims=True)
    return centred * lax.rsqrt(spread + 1e-05) * gain


def position_bias(residue_index_offsets, relative_position_table):
    residue_positions = residue_index_offsets.shape[0]
    heads = relative_position_table.shape[1]
    bins = relative_position_table.shape[0]
    offsets = (
        jnp.clip(residue_index_offsets[None, :] - residue_index_offsets[:, None], -REACH, REACH)
        + REACH
    )
    blocks = offsets.reshape(residue_positions // 64, 64, residue_positions)

    def lookup(block):
        onehot = (block[:, :, None] == jnp.arange(bins, dtype=jnp.int32)[None, None, :]).astype(
            jnp.float32
        )
        return jnp.einsum(
            "ijt,th->ijh", onehot, relative_position_table, precision=lax.Precision.HIGHEST
        )

    table = lax.map(lookup, blocks).reshape(residue_positions, residue_positions, heads)
    return jnp.transpose(table, (2, 0, 1))


def pair_rows(left_blocks, columns, pair_weight, pair_projection_bias, total_seq):
    width = left_blocks.shape[2] // 4
    count = columns.shape[1] // width

    def single(block):
        product = (
            lax.dot_general(
                block, columns, (((0,), (0,)), ((), ())), preferred_element_type=jnp.float32
            )
            / total_seq
        )
        product = jnp.transpose(product.reshape(4, width, count, width), (0, 2, 1, 3)).reshape(
            4 * count, width * width
        )
        product = product.astype(jnp.bfloat16)
        return (
            jnp.dot(product, pair_weight, preferred_element_type=jnp.float32) + pair_projection_bias
        ).reshape(4, count, -1)

    result = lax.map(single, left_blocks)
    return result.reshape(left_blocks.shape[0] * 4, count, -1)


def shards(
    alignment_token_ids,
    residue_index_offsets,
    target_residue_feature,
    token_embedding_table,
    attention_norm_gain,
    query_weight,
    key_weight,
    value_weight,
    gate_weight,
    gate_offset_bias,
    output_weight,
    relative_position_table,
    product_norm_gain,
    left_weight,
    right_weight,
    pair_weight,
    pair_projection_bias,
):
    sequence_local_rows, residue_positions = alignment_token_ids.shape
    devices = lax.axis_size("wide")
    total_seq = sequence_local_rows * devices
    heads = relative_position_table.shape[1]
    head_size = query_weight.shape[1] // heads
    width = left_weight.shape[1]
    onehot = (
        alignment_token_ids[:, :, None]
        == jnp.arange(token_embedding_table.shape[0], dtype=jnp.int32)[None, None, :]
    ).astype(jnp.float32)
    alignment_initial = (
        jnp.einsum("srt,tc->src", onehot, token_embedding_table, precision=lax.Precision.HIGHEST)
        + target_residue_feature[None, :, :]
    )
    offset_bias = position_bias(residue_index_offsets, relative_position_table)

    def row_attention_step(row):
        normed = layer_normalize(row, attention_norm_gain).astype(jnp.bfloat16)
        query = (
            jnp.dot(normed, query_weight, preferred_element_type=jnp.float32) / head_size**0.5
        ).astype(jnp.bfloat16)
        keys = jnp.dot(normed, key_weight, preferred_element_type=jnp.float32).astype(jnp.bfloat16)
        values = jnp.dot(normed, value_weight, preferred_element_type=jnp.float32).astype(
            jnp.bfloat16
        )
        gate = jax.nn.sigmoid(
            jnp.dot(normed, gate_weight, preferred_element_type=jnp.float32) + gate_offset_bias
        )
        query_heads = query.reshape(residue_positions, heads, head_size)
        key_heads = keys.reshape(residue_positions, heads, head_size)
        value_heads = values.reshape(residue_positions, heads, head_size)
        scores = (
            jnp.einsum("ihd,jhd->hij", query_heads, key_heads, preferred_element_type=jnp.float32)
            + offset_bias
        )
        scores = scores - jnp.max(scores, axis=-1, keepdims=True)
        expo = jnp.exp(scores)
        weights = (expo / jnp.sum(expo, axis=-1, keepdims=True)).astype(jnp.bfloat16)
        mixed = jnp.einsum("hij,jhd->ihd", weights, value_heads, preferred_element_type=jnp.float32)
        mixed = (mixed.reshape(residue_positions, heads * head_size) * gate).astype(jnp.bfloat16)
        return row + jnp.dot(mixed, output_weight, preferred_element_type=jnp.float32)

    alignment_updated = lax.map(row_attention_step, alignment_initial)
    normalized_second = (
        layer_normalize(alignment_updated, product_norm_gain)
        .astype(jnp.bfloat16)
        .reshape(sequence_local_rows * residue_positions, -1)
    )
    left = (
        jnp.dot(normalized_second, left_weight, preferred_element_type=jnp.float32)
        .astype(jnp.bfloat16)
        .reshape(sequence_local_rows, residue_positions * width)
    )
    right = (
        jnp.dot(normalized_second, right_weight, preferred_element_type=jnp.float32)
        .astype(jnp.bfloat16)
        .reshape(sequence_local_rows, residue_positions * width)
    )
    left_owned = lax.all_to_all(left, "wide", split_axis=1, concat_axis=0, tiled=True)
    owned = left_owned.shape[1] // width
    left_blocks = jnp.transpose(left_owned.reshape(total_seq, owned // 4, 4 * width), (1, 0, 2))
    right_whole = lax.all_gather(right, "wide", axis=0, tiled=True)
    pair = pair_rows(left_blocks, right_whole, pair_weight, pair_projection_bias, total_seq)
    return (alignment_updated, pair)


def solution(mesh):
    placed = (
        P(("groups", "wide"), None),
        P("groups"),
        P("groups", None),
        P(),
        P(),
        P(),
        P(),
        P(),
        P(),
        P(),
        P(),
        P(),
        P(),
        P(),
        P(),
        P(),
        P(),
    )
    return jax.shard_map(
        shards,
        mesh=mesh,
        in_specs=placed,
        out_specs=(P(("groups", "wide"), None, None), P(("groups", "wide"), None, None)),
        check_vma=False,
    )
```

profile of v0, /device:TPU:69, one launch (start us, length us, event | category | flops | bytes accessed | tf_op | source)
XLA Modules:
  0.0 511.5 jit_solution(9296470528096791751)
XLA Ops:
  9.0 45.8 %while.30 = (s32[]{:T(128)}, f32[8,64,512,8]{2,3,1,0:T(8,128)}, s32[8,64,512]{2,1,0:T(8,128)S(1)}, f32[65,8]{0,1:T(8,128)}, s32[]{:T(128)}) while((s32[]{:T(128)}, f32[8,64,512,8]{2,3,1,0:T(8,128)}, s32[8,64,512]{2,1,0:T(8,128)S(1)}, f32[65,8]{0,1:T(8,128)}, s32[]{:T(128)}) %tuple.52), condition=%wide.region_1.2_spmd, body=%wide.region_0.1_spmd.sunk | while | flops 206602240 | bytes 1446465 | solution.py:34
  9.0 5.8 %fusion.82 = f32[8,64,512,8]{2,3,1,0:T(8,128)} fusion(f32[8,64,512,8]{2,3,1,0:T(8,128)} %get-tuple-element.327, s32[]{:T(128)} %get-tuple-element.326, s32[64,512]{1,0:T(8,128)S(1)} %dynamic-slice_bitcast_fusion.2, f32[65,8]{0,1:T(8,128)} %get-tuple-element.334), kind=kOutput, calls=%fused_computation.4.clone.1 | convolution fusion | flops 206602240 | bytes 1184256 | tf_op jit(solution)/shard_map/while/body/eval_jaxpr/ijt,th->ijh/dot_general | solution.py:30
  14.8 5.7 %fusion.82 = f32[8,64,512,8]{2,3,1,0:T(8,128)} fusion(f32[8,64,512,8]{2,3,1,0:T(8,128)} %get-tuple-element.327, s32[]{:T(128)} %get-tuple-element.326, s32[64,512]{1,0:T(8,128)S(1)} %dynamic-slice_bitcast_fusion.2, f32[65,8]{0,1:T(8,128)} %get-tuple-element.334), kind=kOutput, calls=%fused_computation.4.clone.1 | convolution fusion | flops 206602240 | bytes 1184256 | tf_op jit(solution)/shard_map/while/body/eval_jaxpr/ijt,th->ijh/dot_general | solution.py:30
  20.5 5.7 %fusion.82 = f32[8,64,512,8]{2,3,1,0:T(8,128)} fusion(f32[8,64,512,8]{2,3,1,0:T(8,128)} %get-tuple-element.327, s32[]{:T(128)} %get-tuple-element.326, s32[64,512]{1,0:T(8,128)S(1)} %dynamic-slice_bitcast_fusion.2, f32[65,8]{0,1:T(8,128)} %get-tuple-element.334), kind=kOutput, calls=%fused_computation.4.clone.1 | convolution fusion | flops 206602240 | bytes 1184256 | tf_op jit(solution)/shard_map/while/body/eval_jaxpr/ijt,th->ijh/dot_general | solution.py:30
  26.2 5.7 %fusion.82 = f32[8,64,512,8]{2,3,1,0:T(8,128)} fusion(f32[8,64,512,8]{2,3,1,0:T(8,128)} %get-tuple-element.327, s32[]{:T(128)} %get-tuple-element.326, s32[64,512]{1,0:T(8,128)S(1)} %dynamic-slice_bitcast_fusion.2, f32[65,8]{0,1:T(8,128)} %get-tuple-element.334), kind=kOutput, calls=%fused_computation.4.clone.1 | convolution fusion | flops 206602240 | bytes 1184256 | tf_op jit(solution)/shard_map/while/body/eval_jaxpr/ijt,th->ijh/dot_general | solution.py:30
  31.9 5.7 %fusion.82 = f32[8,64,512,8]{2,3,1,0:T(8,128)} fusion(f32[8,64,512,8]{2,3,1,0:T(8,128)} %get-tuple-element.327, s32[]{:T(128)} %get-tuple-element.326, s32[64,512]{1,0:T(8,128)S(1)} %dynamic-slice_bitcast_fusion.2, f32[65,8]{0,1:T(8,128)} %get-tuple-element.334), kind=kOutput, calls=%fused_computation.4.clone.1 | convolution fusion | flops 206602240 | bytes 1184256 | tf_op jit(solution)/shard_map/while/body/eval_jaxpr/ijt,th->ijh/dot_general | solution.py:30
  37.6 5.7 %fusion.82 = f32[8,64,512,8]{2,3,1,0:T(8,128)} fusion(f32[8,64,512,8]{2,3,1,0:T(8,128)} %get-tuple-element.327, s32[]{:T(128)} %get-tuple-element.326, s32[64,512]{1,0:T(8,128)S(1)} %dynamic-slice_bitcast_fusion.2, f32[65,8]{0,1:T(8,128)} %get-tuple-element.334), kind=kOutput, calls=%fused_computation.4.clone.1 | convolution fusion | flops 206602240 | bytes 1184256 | tf_op jit(solution)/shard_map/while/body/eval_jaxpr/ijt,th->ijh/dot_general | solution.py:30
  43.3 5.7 %fusion.82 = f32[8,64,512,8]{2,3,1,0:T(8,128)} fusion(f32[8,64,512,8]{2,3,1,0:T(8,128)} %get-tuple-element.327, s32[]{:T(128)} %get-tuple-element.326, s32[64,512]{1,0:T(8,128)S(1)} %dynamic-slice_bitcast_fusion.2, f32[65,8]{0,1:T(8,128)} %get-tuple-element.334), kind=kOutput, calls=%fused_computation.4.clone.1 | convolution fusion | flops 206602240 | bytes 1184256 | tf_op jit(solution)/shard_map/while/body/eval_jaxpr/ijt,th->ijh/dot_general | solution.py:30
  49.1 5.7 %fusion.82 = f32[8,64,512,8]{2,3,1,0:T(8,128)} fusion(f32[8,64,512,8]{2,3,1,0:T(8,128)} %get-tuple-element.327, s32[]{:T(128)} %get-tuple-element.326, s32[64,512]{1,0:T(8,128)S(1)} %dynamic-slice_bitcast_fusion.2, f32[65,8]{0,1:T(8,128)} %get-tuple-element.334), kind=kOutput, calls=%fused_computation.4.clone.1 | convolution fusion | flops 206602240 | bytes 1184256 | tf_op jit(solution)/shard_map/while/body/eval_jaxpr/ijt,th->ijh/dot_general | solution.py:30
  54.8 10.0 %copy.31 = f32[8,512,512]{1,2,0:T(8,128)} copy(f32[8,512,512]{2,0,1:T(8,128)} %bitcast.140) | data formatting | bytes 16777216 | tf_op jit(solution)/shard_map/while | solution.py:122
  64.9 3.9 convolution_add_fusion.3
  68.8 149.8 %while.31 = (s32[]{:T(128)}, f32[8,512,256]{2,1,0:T(8,128)}, f32[8,512,256]{2,1,0:T(8,128)}, f32[256]{0:T(256)S(1)}, bf16[256,256]{1,0:T(8,128)(2,1)S(1)}, /*ind...) while((s32[]{:T(128)}, f32[8,512,256]{2,1,0:T(8,128)}, ...), condition=%wide.region_7.8_spmd, body=%wide.region_2.7_spmd.sunk | while | flops 755373568 | bytes 25612928 | solution.py:122
  73.1 4.9 fusion.99
  78.3 6.8 %fusion.100 = f32[8,32,512]{2,1,0:T(8,128)S(1)} fusion(bf16[512,8,32]{0,2,1:T(8,128)(2,1)S(1)} %bitcast.145, f32[8,512]{1,0:T(8,128)S(1)} %fusion.99, f32[8,512,512]{1,2,0:T(8,128)} %get-tuple-element.367, bf16[512,8,32]{0,2,1:T(8,128)(2,1)S(1)} %bitcast.142, bf16[512,8,32]{0,2,1:T(8,128)(2,1)S(1)} %bitcast.144), kind=kOutput, calls=%fused_computation.10.clone.1 | convolution fusion | flops 276828672 | bytes 9715712 | tf_op jit(solution)/shard_map/while/body/eval_jaxpr/hij,jhd->ihd/dot_general | solution.py:118
  91.8 4.9 fusion.99
  97.0 6.8 %fusion.100 = f32[8,32,512]{2,1,0:T(8,128)S(1)} fusion(bf16[512,8,32]{0,2,1:T(8,128)(2,1)S(1)} %bitcast.145, f32[8,512]{1,0:T(8,128)S(1)} %fusion.99, f32[8,512,512]{1,2,0:T(8,128)} %get-tuple-element.367, bf16[512,8,32]{0,2,1:T(8,128)(2,1)S(1)} %bitcast.142, bf16[512,8,32]{0,2,1:T(8,128)(2,1)S(1)} %bitcast.144), kind=kOutput, calls=%fused_computation.10.clone.1 | convolution fusion | flops 276828672 | bytes 9715712 | tf_op jit(solution)/shard_map/while/body/eval_jaxpr/hij,jhd->ihd/dot_general | solution.py:118
  110.6 4.9 fusion.99
  115.7 6.8 %fusion.100 = f32[8,32,512]{2,1,0:T(8,128)S(1)} fusion(bf16[512,8,32]{0,2,1:T(8,128)(2,1)S(1)} %bitcast.145, f32[8,512]{1,0:T(8,128)S(1)} %fusion.99, f32[8,512,512]{1,2,0:T(8,128)} %get-tuple-element.367, bf16[512,8,32]{0,2,1:T(8,128)(2,1)S(1)} %bitcast.142, bf16[512,8,32]{0,2,1:T(8,128)(2,1)S(1)} %bitcast.144), kind=kOutput, calls=%fused_computation.10.clone.1 | convolution fusion | flops 276828672 | bytes 9715712 | tf_op jit(solution)/shard_map/while/body/eval_jaxpr/hij,jhd->ihd/dot_general | solution.py:118
  129.3 4.9 fusion.99
  134.5 6.8 %fusion.100 = f32[8,32,512]{2,1,0:T(8,128)S(1)} fusion(bf16[512,8,32]{0,2,1:T(8,128)(2,1)S(1)} %bitcast.145, f32[8,512]{1,0:T(8,128)S(1)} %fusion.99, f32[8,512,512]{1,2,0:T(8,128)} %get-tuple-element.367, bf16[512,8,32]{0,2,1:T(8,128)(2,1)S(1)} %bitcast.142, bf16[512,8,32]{0,2,1:T(8,128)(2,1)S(1)} %bitcast.144), kind=kOutput, calls=%fused_computation.10.clone.1 | convolution fusion | flops 276828672 | bytes 9715712 | tf_op jit(solution)/shard_map/while/body/eval_jaxpr/hij,jhd->ihd/dot_general | solution.py:118
  148.0 4.9 fusion.99
  153.2 6.8 %fusion.100 = f32[8,32,512]{2,1,0:T(8,128)S(1)} fusion(bf16[512,8,32]{0,2,1:T(8,128)(2,1)S(1)} %bitcast.145, f32[8,512]{1,0:T(8,128)S(1)} %fusion.99, f32[8,512,512]{1,2,0:T(8,128)} %get-tuple-element.367, bf16[512,8,32]{0,2,1:T(8,128)(2,1)S(1)} %bitcast.142, bf16[512,8,32]{0,2,1:T(8,128)(2,1)S(1)} %bitcast.144), kind=kOutput, calls=%fused_computation.10.clone.1 | convolution fusion | flops 276828672 | bytes 9715712 | tf_op jit(solution)/shard_map/while/body/eval_jaxpr/hij,jhd->ihd/dot_general | solution.py:118
  166.8 4.9 fusion.99
  171.9 6.8 %fusion.100 = f32[8,32,512]{2,1,0:T(8,128)S(1)} fusion(bf16[512,8,32]{0,2,1:T(8,128)(2,1)S(1)} %bitcast.145, f32[8,512]{1,0:T(8,128)S(1)} %fusion.99, f32[8,512,512]{1,2,0:T(8,128)} %get-tuple-element.367, bf16[512,8,32]{0,2,1:T(8,128)(2,1)S(1)} %bitcast.142, bf16[512,8,32]{0,2,1:T(8,128)(2,1)S(1)} %bitcast.144), kind=kOutput, calls=%fused_computation.10.clone.1 | convolution fusion | flops 276828672 | bytes 9715712 | tf_op jit(solution)/shard_map/while/body/eval_jaxpr/hij,jhd->ihd/dot_general | solution.py:118
  185.5 4.9 fusion.99
  190.7 6.8 %fusion.100 = f32[8,32,512]{2,1,0:T(8,128)S(1)} fusion(bf16[512,8,32]{0,2,1:T(8,128)(2,1)S(1)} %bitcast.145, f32[8,512]{1,0:T(8,128)S(1)} %fusion.99, f32[8,512,512]{1,2,0:T(8,128)} %get-tuple-element.367, bf16[512,8,32]{0,2,1:T(8,128)(2,1)S(1)} %bitcast.142, bf16[512,8,32]{0,2,1:T(8,128)(2,1)S(1)} %bitcast.144), kind=kOutput, calls=%fused_computation.10.clone.1 | convolution fusion | flops 276828672 | bytes 9715712 | tf_op jit(solution)/shard_map/while/body/eval_jaxpr/hij,jhd->ihd/dot_general | solution.py:118
  204.2 4.9 fusion.99
  209.4 6.8 %fusion.100 = f32[8,32,512]{2,1,0:T(8,128)S(1)} fusion(bf16[512,8,32]{0,2,1:T(8,128)(2,1)S(1)} %bitcast.145, f32[8,512]{1,0:T(8,128)S(1)} %fusion.99, f32[8,512,512]{1,2,0:T(8,128)} %get-tuple-element.367, bf16[512,8,32]{0,2,1:T(8,128)(2,1)S(1)} %bitcast.142, bf16[512,8,32]{0,2,1:T(8,128)(2,1)S(1)} %bitcast.144), kind=kOutput, calls=%fused_computation.10.clone.1 | convolution fusion | flops 276828672 | bytes 9715712 | tf_op jit(solution)/shard_map/while/body/eval_jaxpr/hij,jhd->ihd/dot_general | solution.py:118
  232.6 18.5 %all-to-all-start = ((bf16[8,32,512]{2,0,1:T(8,128)(2,1)}), bf16[8,32,512]{2,0,1:T(8,128)(2,1)S(1)}, u32[]{:S(2)}, u32[]{:S(2)}) async-start(bf16[8,32,512]{2,0,1:T(8,128)(2,1)} %copy.33), calls=%async_computation | async-start | bytes 524288 | tf_op jit(solution)/shard_map/all_to_all | solution.py:138
  251.2 24.5 %all-to-all-done = bf16[8,32,512]{2,0,1:T(8,128)(2,1)S(1)} async-done(((bf16[8,32,512]{2,0,1:T(8,128)(2,1)}), bf16[8,32,512]{2,0,1:T(8,128)(2,1)S(1)}, u32[]{:S(2)}, u32[]{:S(2)}) %all-to-all-start) | async-done | bytes 262176 | tf_op jit(solution)/shard_map/all_to_all | solution.py:138
  275.8 47.0 %all-gather.2.cloned.1.call-done = bf16[256,16384]{1,0:T(8,128)(2,1)} async-done(((bf16[8,16384]{1,0:T(8,128)(2,1)}), bf16[256,16384]{1,0:T(8,128)(2,1)}) %all-gather.2.cloned.1.call-update) | async-done | bytes 8388624 | tf_op jit(solution)/shard_map/all_gather | solution.py:141
  322.8 181.1 %while.32 = (s32[]{:T(128)}, f32[4,4,512,128]{3,2,1,0:T(8,128)}, bf16[4,256,128]{2,1,0:T(8,128)(2,1)S(1)}, bf16[256,16384]{1,0:T(8,128)(2,1)}, bf16[1024,128]{1,0:T(8,128)(2,1)S(1)}, /*index=5*/f32[128]{0:T(128)S(1)}, s32[]{:T(128)}) while((s32[]{:T(128)}, f32[4,4,512,128]{3,2,1,0:T(8,128)}, bf16[4,256,128]{2,1,0:T(8,128)(2,1)S(1)}, ...), condition=%wide.region_11.12_spmd, body=%wide.region_10.11_spmd.sunk | while | flops 1615069184 | bytes 45417552 | solution.py:57
  322.8 6.7 %fusion.106 = bf16[128,16384]{1,0:T(8,128)(2,1)} fusion(bf16[256,16384]{1,0:T(8,128)(2,1)} %get-tuple-element.389, bf16[4,256,128]{2,1,0:T(8,128)(2,1)S(1)} %get-tuple-element.388, s32[]{:T(128)} %get-tuple-element.379), kind=kOutput, calls=%fused_computation.39.clone.1 | convolution fusion | flops 1077936128 | bytes 12648452 | tf_op jit(solution)/shard_map/while/body/eval_jaxpr/dot_general | solution.py:44
  329.5 17.2 %convert_element_type.72 = bf16[4,32,512,32]{3,2,1,0:T(8,128)(2,1)} reshape(bf16[128,16384]{1,0:T(8,128)(2,1)} %fusion.106) | data formatting | bytes 8388608 | tf_op jit(solution)/shard_map/while/body/eval_jaxpr/convert_element_type | solution.py:52
  346.7 15.4 %copy.42 = bf16[4,512,32,32]{1,0,3,2:T(4,128)(2,1)} copy(bf16[4,512,32,32]{3,1,2,0:T(8,128)(2,1)} %bitcast.133) | data formatting | bytes 8388608 | tf_op jit(solution)/shard_map/while/body/eval_jaxpr/convert_element_type | solution.py:52
  362.1 3.6 copy.43
  368.1 6.7 %fusion.106 = bf16[128,16384]{1,0:T(8,128)(2,1)} fusion(bf16[256,16384]{1,0:T(8,128)(2,1)} %get-tuple-element.389, bf16[4,256,128]{2,1,0:T(8,128)(2,1)S(1)} %get-tuple-element.388, s32[]{:T(128)} %get-tuple-element.379), kind=kOutput, calls=%fused_computation.39.clone.1 | convolution fusion | flops 1077936128 | bytes 12648452 | tf_op jit(solution)/shard_map/while/body/eval_jaxpr/dot_general | solution.py:44
  374.7 17.2 %convert_element_type.72 = bf16[4,32,512,32]{3,2,1,0:T(8,128)(2,1)} reshape(bf16[128,16384]{1,0:T(8,128)(2,1)} %fusion.106) | data formatting | bytes 8388608 | tf_op jit(solution)/shard_map/while/body/eval_jaxpr/convert_element_type | solution.py:52
  392.0 15.4 %copy.42 = bf16[4,512,32,32]{1,0,3,2:T(4,128)(2,1)} copy(bf16[4,512,32,32]{3,1,2,0:T(8,128)(2,1)} %bitcast.133) | data formatting | bytes 8388608 | tf_op jit(solution)/shard_map/while/body/eval_jaxpr/convert_element_type | solution.py:52
  407.4 3.6 copy.43
  413.3 6.7 %fusion.106 = bf16[128,16384]{1,0:T(8,128)(2,1)} fusion(bf16[256,16384]{1,0:T(8,128)(2,1)} %get-tuple-element.389, bf16[4,256,128]{2,1,0:T(8,128)(2,1)S(1)} %get-tuple-element.388, s32[]{:T(128)} %get-tuple-element.379), kind=kOutput, calls=%fused_computation.39.clone.1 | convolution fusion | flops 1077936128 | bytes 12648452 | tf_op jit(solution)/shard_map/while/body/eval_jaxpr/dot_general | solution.py:44
  420.0 17.2 %convert_element_type.72 = bf16[4,32,512,32]{3,2,1,0:T(8,128)(2,1)} reshape(bf16[128,16384]{1,0:T(8,128)(2,1)} %fusion.106) | data formatting | bytes 8388608 | tf_op jit(solution)/shard_map/while/body/eval_jaxpr/convert_element_type | solution.py:52
  437.2 15.4 %copy.42 = bf16[4,512,32,32]{1,0,3,2:T(4,128)(2,1)} copy(bf16[4,512,32,32]{3,1,2,0:T(8,128)(2,1)} %bitcast.133) | data formatting | bytes 8388608 | tf_op jit(solution)/shard_map/while/body/eval_jaxpr/convert_element_type | solution.py:52
  452.6 3.6 copy.43
  458.6 6.7 %fusion.106 = bf16[128,16384]{1,0:T(8,128)(2,1)} fusion(bf16[256,16384]{1,0:T(8,128)(2,1)} %get-tuple-element.389, bf16[4,256,128]{2,1,0:T(8,128)(2,1)S(1)} %get-tuple-element.388, s32[]{:T(128)} %get-tuple-element.379), kind=kOutput, calls=%fused_computation.39.clone.1 | convolution fusion | flops 1077936128 | bytes 12648452 | tf_op jit(solution)/shard_map/while/body/eval_jaxpr/dot_general | solution.py:44
  465.3 17.2 %convert_element_type.72 = bf16[4,32,512,32]{3,2,1,0:T(8,128)(2,1)} reshape(bf16[128,16384]{1,0:T(8,128)(2,1)} %fusion.106) | data formatting | bytes 8388608 | tf_op jit(solution)/shard_map/while/body/eval_jaxpr/convert_element_type | solution.py:52
  482.5 15.4 %copy.42 = bf16[4,512,32,32]{1,0,3,2:T(4,128)(2,1)} copy(bf16[4,512,32,32]{3,1,2,0:T(8,128)(2,1)} %bitcast.133) | data formatting | bytes 8388608 | tf_op jit(solution)/shard_map/while/body/eval_jaxpr/convert_element_type | solution.py:52
  497.9 3.6 copy.43
  (151 shorter events, 82.0 us)
Async XLA Ops:
  7.2 57.6 %copy-start = (f32[23,256]{1,0:T(8,128)S(1)}, f32[23,256]{1,0:T(8,128)}, u32[]{:S(2)}) copy-start(f32[23,256]{1,0:T(8,128)} %param.26) | copy-start | bytes 70660
  7.2 315.6 %all-gather.2.cloned.1.call-start = ((), (), s32[]{:S(2)}) async-start(), calls=%async_computation.1 | async-start | bytes 8650752 | tf_op jit(solution)/shard_map/all_gather | solution.py:141
  54.8 10.0 %copy-start.7 = (f32[512,256]{1,0:T(8,128)S(1)}, f32[512,256]{1,0:T(8,128)}, u32[]{:S(2)}) copy-start(f32[512,256]{1,0:T(8,128)} %param.25) | copy-start | bytes 1572868
  54.8 10.0 %copy-start.10 = (s32[8,512]{1,0:T(8,128)S(1)}, s32[8,512]{1,0:T(8,128)}, u32[]{:S(2)}) copy-start(s32[8,512]{1,0:T(8,128)} %param.23) | copy-start | bytes 49156
  64.8 4.0 copy-start.4
  64.8 4.0 copy-start.5
  64.8 4.0 copy-start.6
  64.8 3.9 copy-start.9
  64.8 3.9 copy-start.14
  64.9 3.9 copy-start.15
  64.9 3.9 copy-start.16
  218.6 5.9 %copy-start.13 = (f32[256]{0:T(256)S(1)}, f32[256]{0:T(256)}, u32[]{:S(2)}) copy-start(f32[256]{0:T(256)} %param.35) | copy-start | bytes 3076
  221.5 3.5 copy-start.2
  224.5 1.8 copy-start.11
  226.3 3.2 copy-start.12
  227.6 95.2 %copy-start.3 = (bf16[1024,128]{1,0:T(8,128)(2,1)S(1)}, bf16[1024,128]{1,0:T(8,128)(2,1)}, u32[]{:S(2)}) copy-start(bf16[1024,128]{1,0:T(8,128)(2,1)} %param.38) | copy-start | bytes 786436
  227.6 95.2 %copy-start.8 = (f32[128]{0:T(128)S(1)}, f32[128]{0:T(128)}, u32[]{:S(2)}) copy-start(f32[128]{0:T(128)} %param.39) | copy-start | bytes 1540
  232.6 43.1 %all-to-all-start = ((bf16[8,32,512]{2,0,1:T(8,128)(2,1)}), bf16[8,32,512]{2,0,1:T(8,128)(2,1)S(1)}, u32[]{:S(2)}, u32[]{:S(2)}) async-start(bf16[8,32,512]{2,0,1:T(8,128)(2,1)} %copy.33), calls=%async_computation | async-start | bytes 524288 | tf_op jit(solution)/shard_map/all_to_all | solution.py:138
  503.9 0.7 copy-start.1
Sparse Core Ops, SparseCore 0:
  229.7 93.0 all-gather.1
where the time goes:
time: 517 us; the launch traced here: 511 us
  matrix products  201 us (39%)
  local copies, waits for them, and re-layouts  168 us (32%)
  waiting for transfers between devices  71.6 us (14%)
  other arithmetic  38 us (7%)
  starting transfers between devices  18.6 us (4%)
  between operations  14.3 us (3%)
    convert_element_type x8, local copies, waits for them, and re-layouts, single(): product = product.astype(jnp.bfloat16)  131 us
    dot_general x8, matrix products, row_attention_step(): jnp.einsum('hij,jhd->ihd', weights, value_heads, preferred_element_type=j...  54.2 us
    all_gather x1, waiting for transfers between devices, shards(): right_whole = lax.all_gather(right, 'wide', axis=0, tiled=True)  47 us
    dot_general x8, matrix products, lookup(): jnp.einsum('ijt,th->ijh', onehot, relative_position_table, precision=lax....  45.6 us
    sub x8, matrix products, row_attention_step(): scores = scores - jnp.max(scores, axis=-1, keepdims=True)  39.2 us
    dot_general x4, matrix products, single(): lax.dot_general(block, columns, (((0,), (0,)), ((), ())), preferred_eleme...  26.7 us
    all_to_all x1, waiting for transfers between devices, shards(): lax.all_to_all(left, 'wide', split_axis=1, concat_axis=0, tiled=True)  24.5 us
    all_to_all x1, starting transfers between devices, shards(): lax.all_to_all(left, 'wide', split_axis=1, concat_axis=0, tiled=True)  18.5 us
  transfers between devices with their start and end apart: 2, of which 2 were waited for; matrix products, arithmetic and copies ran while one was open for 0% of the time, Pallas kernels for 0%

commit v1 on v0

v1 whole, which is shorter than its diff:
```python
import functools

import jax
import jax.numpy as jnp
from jax import lax
from jax.experimental import pallas as pl
from jax.experimental.pallas import tpu as pltpu
from jax.sharding import PartitionSpec as P

REACH = 32
LANES = 128
F32 = jnp.float32
BF16 = jnp.bfloat16


def dot(a, b):
    return lax.dot_general(a, b, (((1,), (0,)), ((), ())), preferred_element_type=F32)


def dot_tb(a, b):
    return lax.dot_general(a, b, (((1,), (1,)), ((), ())), preferred_element_type=F32)


def dot_ta(a, b):
    return lax.dot_general(a, b, (((0,), (0,)), ((), ())), preferred_element_type=F32)


def layer_normalize(values, gain):
    center = jnp.mean(values, axis=-1, keepdims=True)
    centred = values - center
    spread = jnp.mean(centred * centred, axis=-1, keepdims=True)
    return centred * lax.rsqrt(spread + 1e-05) * gain


def attention_kernel(
    heads,
    tok_ref,
    pos_row_ref,
    pos_col_ref,
    target_ref,
    emb_ref,
    gain_one_ref,
    wq_ref,
    wk_ref,
    wv_ref,
    wg_ref,
    gb_ref,
    wo_ref,
    table_ref,
    gain_two_ref,
    wl_ref,
    wr_ref,
    au_ref,
    left_ref,
    right_ref,
    bias_ref,
    emb3_ref,
    score_ref,
    prob_ref,
    mixed_ref,
    left_acc,
    right_acc,
):
    seq = pl.program_id(0)
    residues, features = target_ref.shape
    classes = emb_ref.shape[0]
    head_size = features // heads
    per_half = LANES // head_size

    @pl.when(seq == 0)
    def _():
        @pl.loop(0, residues // 8)
        def _(block):
            rows = pl.ds(pl.multiple_of(block * 8, 8), 8)
            delta = pos_row_ref[...] - pos_col_ref[rows, :]
            offs = jnp.clip(delta, -REACH, REACH) + REACH
            for h in range(heads):
                source = jnp.broadcast_to(table_ref[h : h + 1, :], (8, LANES))
                for col in range(residues // LANES):
                    cols = slice(col * LANES, (col + 1) * LANES)
                    bias_ref[h, rows, cols] = jnp.take_along_axis(
                        source, offs[:, cols], axis=1, mode="promise_in_bounds"
                    )

        emb3_ref[...] = jnp.zeros_like(emb3_ref)
        rest = emb_ref[...]
        for part in range(3):
            piece = rest.astype(BF16)
            emb3_ref[part * 32 : part * 32 + classes, :] = piece
            rest = rest - piece.astype(F32)
        left_acc[...] = jnp.zeros_like(left_acc)

    token = tok_ref[pl.ds(seq, 1), :]
    klass = lax.broadcasted_iota(jnp.int32, (LANES, residues), 0)
    onehot = jnp.where((klass % 32 == token) & (klass < 96), 1.0, 0.0).astype(BF16)
    start = dot_ta(onehot, emb3_ref[...]) + target_ref[...]
    normed = layer_normalize(start, gain_one_ref[...]).astype(BF16)
    query = (dot(normed, wq_ref[...]) * (1.0 / head_size**0.5)).astype(BF16)
    keys = dot(normed, wk_ref[...]).astype(BF16)
    values = dot(normed, wv_ref[...]).astype(BF16)
    lane = lax.broadcasted_iota(jnp.int32, (residues, features), 1) // head_size
    half_lane = lax.broadcasted_iota(jnp.int32, (residues, LANES), 1) // head_size
    ones = jnp.ones((residues, LANES), BF16)
    for h in range(heads):
        half, place = divmod(h, per_half)
        masked = jnp.where(lane == h, query, jnp.zeros_like(query))
        score_ref[h % 2] = dot_tb(masked, keys)
        for block in range(residues // LANES):
            rows = slice(block * LANES, (block + 1) * LANES)
            scores = score_ref[h % 2, rows, :] + bias_ref[h, rows, :]
            peak = jnp.max(scores, axis=1, keepdims=True)
            prob_ref[h % 2, rows, :] = jnp.exp(scores - peak).astype(BF16)
        extended = jnp.concatenate([values[:, half * LANES : (half + 1) * LANES], ones], axis=1)
        product = dot(prob_ref[h % 2], extended)
        result = product[:, :LANES] / product[:, LANES:]
        cols = slice(half * LANES, (half + 1) * LANES)
        if place == 0:
            mixed_ref[:, cols] = result
        else:
            mixed_ref[:, cols] = jnp.where(half_lane == place, result, mixed_ref[:, cols])
    gate = jax.nn.sigmoid(dot(normed, wg_ref[...]) + gb_ref[...])
    mixed = (mixed_ref[...] * gate).astype(BF16)
    updated = start + dot(mixed, wo_ref[...])
    au_ref[0] = updated
    second = layer_normalize(updated, gain_two_ref[...]).astype(BF16)
    group = seq // 4
    rows = pl.ds(pl.multiple_of(group * residues, residues), residues)
    left_acc[rows, :] += dot(second, wl_ref[seq % 4])
    right = dot_tb(wr_ref[...], second)
    for col in range(residues // LANES):
        right_acc[col, pl.ds(seq, 32, stride=8), :] = right[:, col * LANES : (col + 1) * LANES]

    @pl.when(seq == pl.num_programs(0) - 1)
    def _():
        devices, groups, owned, _ = left_ref.shape
        for g in range(groups):
            part = left_acc[g * residues : (g + 1) * residues, :].astype(BF16)
            left_ref[:, g] = part.reshape(devices, owned, LANES)
        for col in range(residues // LANES):
            right_ref[:, col * LANES : (col + 1) * LANES] = right_acc[col].astype(BF16)


def attention(
    devices,
    tokens,
    positions,
    target,
    emb,
    gain_one,
    wq,
    wk,
    wv,
    wg,
    gb,
    wo,
    table,
    gain_two,
    wl,
    wr,
):
    sequences, residues = tokens.shape
    features = target.shape[1]
    heads = table.shape[1]
    width = wl.shape[1]
    table_rows = jnp.pad(table.T, ((0, 0), (0, LANES - table.shape[0])))
    wl4 = jnp.stack([jnp.pad(wl, ((0, 0), (k * width, LANES - (k + 1) * width))) for k in range(4)])
    operands = (
        tokens,
        positions[None, :],
        positions[:, None],
        target,
        emb,
        gain_one[None, :],
        wq,
        wk,
        wv,
        wg,
        gb[None, :],
        wo,
        table_rows,
        gain_two[None, :],
        wl4,
        wr.T,
    )
    owned = residues // devices

    def const(a):
        return pl.BlockSpec(a.shape, lambda s: (0,) * a.ndim)

    return pl.pallas_call(
        functools.partial(attention_kernel, heads),
        grid=(sequences,),
        in_specs=[const(a) for a in operands],
        out_specs=(
            pl.BlockSpec((1, residues, features), lambda s: (s, 0, 0)),
            pl.BlockSpec((devices, 2, owned, LANES), lambda s: (0, 0, 0, 0)),
            pl.BlockSpec((width * sequences, residues), lambda s: (0, 0)),
        ),
        out_shape=(
            jax.ShapeDtypeStruct((sequences, residues, features), F32),
            jax.ShapeDtypeStruct((devices, 2, owned, LANES), BF16),
            jax.ShapeDtypeStruct((width * sequences, residues), BF16),
        ),
        scratch_shapes=[
            pltpu.VMEM((heads, residues, residues), F32),
            pltpu.VMEM((LANES, features), BF16),
            pltpu.VMEM((2, residues, residues), F32),
            pltpu.VMEM((2, residues, residues), BF16),
            pltpu.VMEM((residues, features), F32),
            pltpu.VMEM((2 * residues, LANES), F32),
            pltpu.VMEM((residues // LANES, width * sequences, LANES), F32),
        ],
        compiler_params=pltpu.CompilerParams(
            dimension_semantics=("arbitrary",), vmem_limit_bytes=60 << 20
        ),
        cost_estimate=pl.CostEstimate(
            flops=20_000_000_000, bytes_accessed=8 << 20, transcendentals=17_000_000
        ),
        name="row_attention",
    )(*operands)


def exchange_kernel(
    devices,
    chunks,
    lag,
    left_ref,
    right_ref,
    weight_ref,
    bias_ref,
    pair_ref,
    held_ref,
    left_held,
    left_wide,
    left_rows,
    y_ref,
    acc_ref,
    send_sem,
    up_sem,
    down_sem,
    mate_sem,
    left_send_sem,
    left_recv_sem,
):
    me = lax.axis_index("wide")
    rings = devices // 2
    place, core = me // 2, lax.rem(me, 2)
    mine = core * rings
    up = lax.rem(place + 1, rings) * 2 + core
    down = lax.rem(place + rings - 1, rings) * 2 + core
    mate = place * 2 + 1 - core
    owned, residues, _ = pair_ref.shape
    rows = right_ref.shape[0] // chunks
    total = left_rows.shape[1]
    width = left_rows.shape[0] // owned
    per_chunk = rows // 8
    far = rings // 2

    barrier = pltpu.get_barrier_semaphore()

    @pl.loop(1, devices)
    def _(r):
        pl.semaphore_signal(
            barrier,
            inc=1,
            device_id={"wide": lax.rem(me + r, devices)},
            device_id_type=pl.DeviceIdType.MESH,
        )

    pl.semaphore_wait(barrier, devices - 1)

    def copy(src, k, slot, sem, target):
        return pltpu.make_async_remote_copy(
            src_ref=src,
            dst_ref=held_ref.at[k * devices + slot],
            send_sem=send_sem,
            recv_sem=sem,
            device_id={"wide": target},
            device_id_type=pl.DeviceIdType.MESH,
        )

    def reach(k):
        return (far, far - 1) if k % 2 == 0 else (far - 1, far)

    def step(k, t):
        ups, downs = reach(k)
        if t == 0:
            own = right_ref.at[pl.ds(k * rows, rows)]
            slot = mine + place
            copy(own, k, slot, up_sem.at[k, 0], up).start()
            copy(own, k, slot, down_sem.at[k, 0], down).start()
            copy(own, k, slot, mate_sem.at[k], mate).start()
            return
        for sem, reached, origin, target in (
            (up_sem, ups, place + rings - t, up),
            (down_sem, downs, place + t, down),
        ):
            if t > reached:
                continue
            slot = mine + lax.rem(origin, rings)
            block = held_ref.at[k * devices + slot]
            copy(block, k, slot, sem.at[k, t - 1], target).wait_recv()
            if t < reached:
                copy(block, k, slot, sem.at[k, t], target).start()
            copy(block, k, slot, mate_sem.at[k], mate).start()

    def send_left():
        @pl.loop(1, devices)
        def _(r):
            target = lax.rem(me + r, devices)
            pltpu.make_async_remote_copy(
                src_ref=left_ref.at[target],
                dst_ref=left_held.at[mine + place],
                send_sem=left_send_sem,
                recv_sem=left_recv_sem,
                device_id={"wide": target},
                device_id_type=pl.DeviceIdType.MESH,
            ).start()

    def left_copies():
        return pltpu.make_async_remote_copy(
            src_ref=left_held.at[pl.ds(0, devices - 1)],
            dst_ref=left_held.at[pl.ds(0, devices - 1)],
            send_sem=left_send_sem,
            recv_sem=left_recv_sem,
            device_id={"wide": mate},
            device_id_type=pl.DeviceIdType.MESH,
        )

    def arrange_left():
        left_copies().wait_recv()
        left_held[mine + place] = left_ref[me]
        left_wide[...] = left_held[...].astype(F32).reshape(left_wide.shape)
        blocks = 2 * devices
        lane = lax.broadcasted_iota(jnp.int32, (blocks, total), 1)
        spread = jnp.where(
            lane // 4 == lax.broadcasted_iota(jnp.int32, (blocks, total), 0), 1.0, 0.0
        ).astype(BF16)
        column = lax.rem(lax.broadcasted_iota(jnp.int32, (width, total), 1), 4)
        for i in range(owned):
            block = left_wide[pl.ds(i, blocks, stride=owned), :].astype(BF16)
            lifted = dot_ta(block, spread)
            rows_i = lifted[:width]
            for s in range(1, 4):
                rows_i = jnp.where(column == s, lifted[s * width : (s + 1) * width], rows_i)
            left_rows[i * width : (i + 1) * width, :] = rows_i.astype(BF16)

    def arrived(k):
        theirs = held_ref.at[pl.ds(k * devices + (1 - core) * rings, rings)]
        pltpu.make_async_remote_copy(
            src_ref=theirs,
            dst_ref=theirs,
            send_sem=send_sem,
            recv_sem=mate_sem.at[k],
            device_id={"wide": mate},
            device_id_type=pl.DeviceIdType.MESH,
        ).wait_recv()
        held_ref[k * devices + mine + place] = right_ref[pl.ds(k * rows, rows), :]

    def products(k, two):
        first = slice(two * 16, two * 16 + 16)
        block = held_ref[pl.ds(k * devices, devices), first, :].astype(F32)
        for which in range(2):
            e = two * 2 + which
            right = block[:, which * 8 : which * 8 + 8, :].reshape(total, residues).astype(BF16)
            product = dot(left_rows[...], right).astype(BF16)
            y_ref[:, e * width : (e + 1) * width, :] = product.reshape(owned, width, residues)

    def project(k, start, count):
        columns = slice(k * per_chunk * width, (k + 1) * per_chunk * width)
        for i in range(start, start + count):
            part = dot(weight_ref[:, columns], y_ref[i])
            if k > 0:
                part = part + acc_ref[i]
            if k < chunks - 1:
                acc_ref[i] = part
            else:
                pair_ref[i] = part.T * (1.0 / total) + bias_ref[...]

    def pieces(k):
        yield functools.partial(arrived, k)
        for two in range(per_chunk // 2):
            yield functools.partial(products, k, two)
        for start in range(0, owned, 4):
            yield functools.partial(project, k, start, 4)

    pending = []
    last = lag * (chunks - 1) + far
    for tick in range(last + 1):
        for k in range(chunks):
            t = tick - lag * k
            if 0 <= t <= far:
                step(k, t)
                if t == far:
                    pending.extend(pieces(k))
        if tick == 0:
            send_left()
        if tick == far - 1:
            arrange_left()
        for _ in range(5):
            if pending:
                pending.pop(0)()
    for piece in pending:
        piece()
    left_copies().wait_send()
    everything = held_ref.at[pl.ds(0, chunks * (devices - 1))]
    pltpu.make_async_remote_copy(
        src_ref=everything,
        dst_ref=everything,
        send_sem=send_sem,
        recv_sem=mate_sem.at[0],
        device_id={"wide": mate},
        device_id_type=pl.DeviceIdType.MESH,
    ).wait_send()


def exchange(devices, left, right, pair_weight, pair_bias):
    _, groups, owned, _ = left.shape
    rows, residues = right.shape
    width = rows // 8
    channels = pair_weight.shape[1]
    total = devices * 8
    chunks = 4
    rings = devices // 2
    weight = jnp.transpose(pair_weight.reshape(width, width, channels), (2, 1, 0)).reshape(
        channels, width * width
    )
    whole = pl.BlockSpec(memory_space=pltpu.VMEM)
    return pl.pallas_call(
        functools.partial(exchange_kernel, devices, chunks, 2),
        in_specs=[whole] * 4,
        out_specs=whole,
        out_shape=jax.ShapeDtypeStruct((owned, residues, channels), F32),
        scratch_shapes=[
            pltpu.VMEM((chunks * devices, rows // chunks, residues), BF16),
            pltpu.VMEM((devices, groups, owned, LANES), BF16),
            pltpu.VMEM((devices * groups * owned, LANES), F32),
            pltpu.VMEM((owned * width, total), BF16),
            pltpu.VMEM((owned, (width // chunks) * width, residues), BF16),
            pltpu.VMEM((owned, channels, residues), F32),
            pltpu.SemaphoreType.DMA,
            pltpu.SemaphoreType.DMA((chunks, rings // 2)),
            pltpu.SemaphoreType.DMA((chunks, rings // 2)),
            pltpu.SemaphoreType.DMA((chunks,)),
            pltpu.SemaphoreType.DMA,
            pltpu.SemaphoreType.DMA,
        ],
        compiler_params=pltpu.CompilerParams(
            collective_id=0, has_side_effects=True, vmem_limit_bytes=48 << 20
        ),
        cost_estimate=pl.CostEstimate(
            flops=7_000_000_000, bytes_accessed=12 << 20, transcendentals=0
        ),
        name="exchange_outer",
    )(left, right, weight, pair_bias[None, :])


def shards(
    alignment_token_ids,
    residue_index_offsets,
    target_residue_feature,
    token_embedding_table,
    attention_norm_gain,
    query_weight,
    key_weight,
    value_weight,
    gate_weight,
    gate_offset_bias,
    output_weight,
    relative_position_table,
    product_norm_gain,
    left_weight,
    right_weight,
    pair_weight,
    pair_projection_bias,
):
    devices = lax.axis_size("wide")
    updated, left, right = attention(
        devices,
        alignment_token_ids,
        residue_index_offsets,
        target_residue_feature,
        token_embedding_table,
        attention_norm_gain,
        query_weight,
        key_weight,
        value_weight,
        gate_weight,
        gate_offset_bias,
        output_weight,
        relative_position_table,
        product_norm_gain,
        left_weight,
        right_weight,
    )
    pair = exchange(devices, left, right, pair_weight, pair_projection_bias)
    return (updated, pair)


def solution(mesh):
    placed = (
        P(("groups", "wide"), None),
        P("groups"),
        P("groups", None),
    ) + (P(),) * 14
    return jax.shard_map(
        shards,
        mesh=mesh,
        in_specs=placed,
        out_specs=(P(("groups", "wide"), None, None), P(("groups", "wide"), None, None)),
        check_vma=False,
    )
```

time: 517 us -> 148 us (0.29); the launches traced: 511 us -> 148 us
  matrix products: 201 us -> 0 us
  local copies, waits for them, and re-layouts: 168 us -> 8.89 us
  Pallas kernels: 0 us -> 138 us
  waiting for transfers between devices: 71.6 us -> 0 us
  other arithmetic: 38 us -> 0.73 us
  starting transfers between devices: 18.6 us -> 0 us
  between operations: 14.3 us -> 0.67 us
    dot_general x59 -> x0, matrix products: 162 us -> none  [the longest x8 54.2 us: row_attention_step(): jnp.einsum('hij,jhd->ihd', weights, value_heads, preferred_element_type=j...]
    pallas_call x0 -> x2, Pallas kernels: none -> 138 us  [the longest x1 88.8 us: exchange(): pl.pallas_call(functools.partial(exchange_kernel, devices, chunks, 2), in...]
    convert_element_type x10 -> x0, local copies, waits for them, and re-layouts: 132 us -> none  [the longest x8 131 us: single(): product = product.astype(jnp.bfloat16)]
    all_gather x1 -> x0, waiting for transfers between devices: 47 us -> none  [shards(): right_whole = lax.all_gather(right, 'wide', axis=0, tiled=True)]
    sub x8 -> x0, matrix products: 39.2 us -> none  [row_attention_step(): scores = scores - jnp.max(scores, axis=-1, keepdims=True)]
    reduce_sum x18 -> x0, other arithmetic: 25.5 us -> none  [the longest x9 13.2 us: layer_normalize(): spread = jnp.mean(centred * centred, axis=-1, keepdims=True)]
    all_to_all x1 -> x0, waiting for transfers between devices: 24.5 us -> none  [shards(): lax.all_to_all(left, 'wide', split_axis=1, concat_axis=0, tiled=True)]
    while x6 -> x0, local copies, waits for them, and re-layouts: 24.4 us -> none
  transfers between devices with their start and end apart: 2 -> 0, of which waited for: 2 -> 0; matrix products, arithmetic and copies ran while one was open for 0% -> 0% of each run, Pallas kernels for 0% -> 0%
where the time goes in v1:
time: 148 us
  Pallas kernels  138 us (93%)
  local copies, waits for them, and re-layouts  8.89 us (6%)
    pallas_call x1, Pallas kernels, exchange(): pl.pallas_call(functools.partial(exchange_kernel, devices, chunks, 2), in...  88.8 us
    pallas_call x1, Pallas kernels, attention(): pl.pallas_call(functools.partial(attention_kernel, heads), grid=(sequence...  48.7 us
    unnamed x8, local copies, waits for them, and re-layouts  4.75 us

profile of v1, /device:TPU:69, one launch (start us, length us, event | category | flops | bytes accessed | tf_op | source)
XLA Modules:
  0.0 147.8 jit_solution(1898045744275272722)
XLA Ops:
  0.6 1.3 pad.20.table_ref
  1.9 0.8 copy.30
  2.7 0.1 pad_bitcast_fusion.3
  2.9 0.7 pad_maximum_fusion.wl_ref
  3.6 1.1 copy.35
  4.7 0.1 copy.36.weight_ref
  4.8 1.5 %copy.34.pos_col_ref = s32[512,1]{1,0:T(8,128)} copy(s32[512,1]{0,1:T(1,128)} %bitcast.24) | data formatting | bytes 4096 | tf_op jit(solution)/shard_map/broadcast_in_dim | solution.py:170
  6.4 0.0 copy-start
  6.4 48.7 %row_attention.1 = (f32[8,512,256]{2,1,0:T(8,128)}, bf16[32,2,16,128]{3,2,1,0:T(8,128)(2,1)}, bf16[256,512]{1,0:T(8,128)(2,1)}) custom-call(s32[8,512]{1,0:T(8,128)} %tok_ref.1, s32[1,512]{1,0:T(1,128)} %bitcast.25, s32[512,1]{1,0:T(8,128)} %copy.34.pos_col_ref, f32[512,256]{1,0:T(8,128)} %target_ref.1, f32[23,256]{1,0:T(8,128)} %emb_ref.1, ...), custom_call_target="tpu_custom_call" | custom-call | flops 20000000000 | bytes 8388608 | tf_op jit(solution)/shard_map/row_attention/pallas_call | solution.py:190
  55.1 0.0 copy-done
  55.1 0.0 copy-start.1
  55.1 0.9 copy-done.1
  56.1 0.0 copy-start.2
  56.1 0.9 copy-done.2
  57.0 88.8 %exchange_outer.1 = f32[16,512,128]{2,1,0:T(8,128)S(1)} custom-call(bf16[32,2,16,128]{3,2,1,0:T(8,128)(2,1)S(1)} %copy-done.1, bf16[256,512]{1,0:T(8,128)(2,1)S(1)} %copy-done.2, bf16[128,1024]{1,0:T(8,128)(2,1)S(1)} %copy.36.weight_ref, f32[1,128]{1,0:T(1,128)S(1)} %bitcast.20), custom_call_target="tpu_custom_call" | custom-call | flops 7000000000 | bytes 12582912 | tf_op jit(solution)/shard_map/exchange_outer/pallas_call | solution.py:429
  145.8 2.0 %copy.38 = f32[16,512,128]{2,1,0:T(8,128)} copy(f32[16,512,128]{2,1,0:T(8,128)S(1)} %exchange_outer.1) | data formatting | bytes 8388608
Async XLA Ops:
  6.4 48.8 %copy-start = (f32[128]{0:T(128)S(1)}, f32[128]{0:T(128)}, u32[]{:S(2)}) copy-start(f32[128]{0:T(128)} %param.33) | copy-start | bytes 1540
  55.1 1.0 copy-start.1
  56.1 0.9 copy-start.2

commit v2 on v0

v2 whole, which is shorter than its diff:
```python
import functools

import jax
import jax.numpy as jnp
from jax import lax
from jax.experimental import pallas as pl
from jax.experimental.pallas import tpu as pltpu
from jax.sharding import PartitionSpec as P

REACH = 32
LANES = 128
F32 = jnp.float32
BF16 = jnp.bfloat16


def dot(a, b):
    return lax.dot_general(a, b, (((1,), (0,)), ((), ())), preferred_element_type=F32)


def dot_tb(a, b):
    return lax.dot_general(a, b, (((1,), (1,)), ((), ())), preferred_element_type=F32)


def dot_ta(a, b):
    return lax.dot_general(a, b, (((0,), (0,)), ((), ())), preferred_element_type=F32)


def layer_normalize(values, gain):
    center = jnp.mean(values, axis=-1, keepdims=True)
    centred = values - center
    spread = jnp.mean(centred * centred, axis=-1, keepdims=True)
    return centred * lax.rsqrt(spread + 1e-05) * gain


GROUPS = 2
CHUNKS = 4
STARTS = (0, 0, 1, 1)


def block_kernel(
    devices,
    heads,
    tok_ref,
    pos_row_ref,
    target_ref,
    emb_ref,
    gain_one_ref,
    wq_ref,
    wk_ref,
    wv_ref,
    wg_ref,
    gb_ref,
    wo_ref,
    table_ref,
    gain_two_ref,
    wl_ref,
    wr_ref,
    raw_weight_ref,
    pair_bias_ref,
    au_ref,
    pair_ref,
    bias_ref,
    turn_ref,
    wl4_ref,
    wr4_ref,
    wide_weight,
    weight_ref,
    emb3_ref,
    score_ref,
    prob_ref,
    mixed_ref,
    left_acc,
    right_acc,
    left_out,
    left_held,
    left_wide,
    left_rows,
    held_ref,
    y_ref,
    acc_ref,
    send_sem,
    up_sem,
    down_sem,
    mate_sem,
    left_send_sem,
    left_recv_sem,
):
    seq = pl.program_id(0)
    sequences = tok_ref.shape[0]
    share = sequences // GROUPS
    residues, features = target_ref.shape
    classes = emb_ref.shape[0]
    head_size = features // heads
    per_half = LANES // head_size
    owned = pair_ref.shape[0]
    width = right_acc.shape[1] // sequences
    group_rows = width * share
    rows = group_rows // CHUNKS
    total = left_rows.shape[2]
    per_chunk = width // CHUNKS

    me = lax.axis_index("wide")
    rings = devices // 2
    place, core = me // 2, lax.rem(me, 2)
    mine = core * rings
    up = lax.rem(place + 1, rings) * 2 + core
    down = lax.rem(place + rings - 1, rings) * 2 + core
    mate = place * 2 + 1 - core
    far = rings // 2
    swap = lax.rem(place, 2) * 2

    barrier = pltpu.get_barrier_semaphore()

    @pl.when(seq == 0)
    def _():
        @pl.loop(1, devices)
        def _(r):
            pl.semaphore_signal(
                barrier,
                inc=1,
                device_id={"wide": lax.rem(me + r, devices)},
                device_id_type=pl.DeviceIdType.MESH,
            )

    @pl.when(seq == share - 1)
    def _():
        pl.semaphore_wait(barrier, devices - 1)

    def remote(src, dst, send, recv, target):
        return pltpu.make_async_remote_copy(
            src_ref=src,
            dst_ref=dst,
            send_sem=send,
            recv_sem=recv,
            device_id={"wide": target},
            device_id_type=pl.DeviceIdType.MESH,
        )

    def reach(k):
        return (far, far - 1) if k % 2 == 0 else (far - 1, far)

    def step(g, k, t):
        base = (g * CHUNKS + k) * devices
        which = g * CHUNKS + k
        ups, downs = reach(k)

        def begin():
            own = held_ref.at[base + mine + place]
            remote(own, own, send_sem, up_sem.at[which, 0], up).start()
            remote(own, own, send_sem, down_sem.at[which, 0], down).start()
            remote(own, own, send_sem, mate_sem.at[which], mate).start()

        def forward():
            for sem, reached, origin, target in (
                (up_sem, ups, place + rings - t, up),
                (down_sem, downs, place + t, down),
            ):
                if isinstance(t, int) and t > reached:
                    continue
                item = held_ref.at[base + mine + lax.rem(origin, rings)]
                remote(item, item, send_sem, sem.at[which, t - 1], target).wait_recv()

                def onward(item=item, sem=sem, target=target):
                    remote(item, item, send_sem, sem.at[which, t], target).start()
                if not isinstance(t, int):
                    pl.when(t < reached)(onward)
                elif t < reached:
                    onward()
                remote(item, item, send_sem, mate_sem.at[which], mate).start()

        if isinstance(t, int):
            begin() if t == 0 else forward()
        else:
            pl.when(t == 0)(begin)
            pl.when(t > 0)(forward)

    def send_left(g):
        @pl.loop(1, devices)
        def _(r):
            target = lax.rem(me + r, devices)
            remote(
                left_out.at[g * devices + target],
                left_held.at[g * devices + mine + place],
                left_send_sem,
                left_recv_sem.at[g],
                target,
            ).start()

    def ring_slot(slot):
        @pl.when(seq >= share)
        def _():
            t = (seq - share) * 2 + slot // 2
            for k in range(CHUNKS):
                if k // 2 == slot % 2:
                    step(0, k, t)
            if slot == 0:
                pl.when(seq == share)(functools.partial(send_left, 0))

    @pl.when(seq == 0)
    def _():
        turn_ref[...] = jnp.zeros_like(turn_ref)
        turn_ref[:, : table_ref.shape[1]] = table_ref[...]
        table_rows = turn_ref[...]
        spots = pos_row_ref[...].astype(F32)
        tiles = residues // LANES
        for tile in range(tiles):
            cols = slice(tile * LANES, (tile + 1) * LANES)
            across = jnp.broadcast_to(spots[:, cols], (LANES, LANES))
            down_rows = across.T
            for sub in range(LANES // REACH):
                span = slice(tile * LANES + sub * REACH, tile * LANES + (sub + 1) * REACH)
                own = down_rows[sub * REACH : (sub + 1) * REACH, :]
                for other in range(tiles):
                    dst = slice(other * LANES, (other + 1) * LANES)
                    near = (
                        other == tile
                        or (other == tile - 1 and sub == 0)
                        or (other == tile + 1 and sub == LANES // REACH - 1)
                    )
                    if near:
                        delta = jnp.broadcast_to(spots[:, dst], (REACH, LANES)) - own
                        offs = (jnp.clip(delta, -REACH, REACH) + REACH).astype(jnp.int32)
                    for h in range(heads):
                        row = table_rows[h : h + 1, :]
                        if near:
                            bias_ref[h, span, dst] = jnp.take_along_axis(
                                jnp.broadcast_to(row, (REACH, LANES)),
                                offs,
                                axis=1,
                                mode="promise_in_bounds",
                            )
                        else:
                            edge = row[:, 2 * REACH : 2 * REACH + 1] if other > tile else row[:, :1]
                            bias_ref[h, span, dst] = jnp.broadcast_to(edge, (REACH, LANES))

        wl4_ref[...] = jnp.zeros_like(wl4_ref)
        for k in range(share):
            wl4_ref[k, k * width : (k + 1) * width, :] = wl_ref[...]
        for col in range(features // LANES):
            wr4_ref[0, col] = wr_ref[:, col * LANES : (col + 1) * LANES].astype(F32)
        for x in range(1, 4):
            for p in range(4):
                for col in range(features // LANES):
                    wr4_ref[x, col, pl.ds(p, width // 4, stride=4), :] = wr4_ref[
                        0, col, pl.ds(p ^ x, width // 4, stride=4), :
                    ]

        emb3_ref[...] = jnp.zeros_like(emb3_ref)
        rest = emb_ref[...]
        for part in range(3):
            piece = rest.astype(BF16)
            emb3_ref[part * 32 : part * 32 + classes, :] = piece
            rest = rest - piece.astype(F32)
        left_acc[...] = jnp.zeros_like(left_acc)

    token = tok_ref[pl.ds(seq, 1), :]
    klass = lax.broadcasted_iota(jnp.int32, (LANES, residues), 0)
    onehot = jnp.where((klass % 32 == token) & (klass < 96), 1.0, 0.0).astype(BF16)
    start = dot_ta(onehot, emb3_ref[...]) + target_ref[...]
    normed = layer_normalize(start, gain_one_ref[...]).astype(BF16)
    query = (dot(normed, wq_ref[...]) * (1.0 / head_size**0.5)).astype(BF16)
    keys = dot(normed, wk_ref[...]).astype(BF16)
    values = dot(normed, wv_ref[...]).astype(BF16)
    lane = lax.broadcasted_iota(jnp.int32, (residues, features), 1) // head_size
    half_lane = lax.broadcasted_iota(jnp.int32, (residues, LANES), 1) // head_size
    ones = jnp.ones((residues, LANES), BF16)

    def score(h):
        masked = jnp.where(lane == h, query, jnp.zeros_like(query))
        score_ref[h % 4] = dot_tb(masked, keys)

    def soften(h):
        for piece in range(residues // LANES):
            span = slice(piece * LANES, (piece + 1) * LANES)
            scores = score_ref[h % 4, span, :] + bias_ref[h, span, :]
            peak = jnp.max(scores, axis=1, keepdims=True)
            prob_ref[h % 4, span, :] = jnp.exp(scores - peak).astype(BF16)

    def mix(h):
        half, spot = divmod(h, per_half)
        cols = slice(half * LANES, (half + 1) * LANES)
        product = dot(prob_ref[h % 4], jnp.concatenate([values[:, cols], ones], axis=1))
        result = product[:, :LANES] / product[:, LANES:]
        if spot == 0:
            mixed_ref[:, cols] = result
        else:
            mixed_ref[:, cols] = jnp.where(half_lane == spot, result, mixed_ref[:, cols])

    stages = heads // 2
    score(0)
    score(1)
    for stage in range(stages):
        for which in range(2):
            if stage + 1 < stages:
                score(stage * 2 + 2 + which)
            soften(stage * 2 + which)
            if stage > 0:
                mix(stage * 2 - 2 + which)
        ring_slot(stage)
    mix(heads - 2)
    mix(heads - 1)

    gate = jax.nn.sigmoid(dot(normed, wg_ref[...]) + gb_ref[...])
    mixed = (mixed_ref[...] * gate).astype(BF16)
    updated = start + dot(mixed, wo_ref[...])
    au_ref[0] = updated
    second = layer_normalize(updated, gain_two_ref[...]).astype(BF16)
    group = seq // share
    member = lax.rem(seq, share)
    span = pl.ds(pl.multiple_of(group * residues, residues), residues)
    left_acc[span, :] += dot_tb(second, wl4_ref[member])
    parts = [wr4_ref[swap + group, col] for col in range(features // LANES)]
    right = dot_tb(jnp.concatenate(parts, axis=1).astype(BF16), second)
    for col in range(residues // LANES):
        right_acc[col, pl.ds(group * group_rows + member, width, stride=share), :] = right[
            :, col * LANES : (col + 1) * LANES
        ]

    def finish_group(g):
        part = left_acc[g * residues : (g + 1) * residues, :].astype(BF16)
        left_out[g * devices : (g + 1) * devices] = part.reshape(devices, owned, LANES)
        for k in range(CHUNKS):
            first = g * group_rows + k * rows
            for col in range(residues // LANES):
                held_ref[
                    (g * CHUNKS + k) * devices + mine + place,
                    :,
                    col * LANES : (col + 1) * LANES,
                ] = right_acc[col, first : first + rows, :].astype(BF16)

    for g in range(GROUPS):
        pl.when(seq == (g + 1) * share - 1)(functools.partial(finish_group, g))

    def arrange_left():
        for g in range(GROUPS):
            arrived = left_held.at[pl.ds(g * devices, devices - 1)]
            remote(arrived, arrived, left_send_sem, left_recv_sem.at[g], mate).wait_recv()
            left_held[g * devices + mine + place] = left_out[g * devices + me]
        left_wide[...] = left_held[...].astype(F32).reshape(left_wide.shape)
        blocks = GROUPS * devices
        block_id = lax.broadcasted_iota(jnp.int32, (blocks, total), 0)
        lane_id = lax.broadcasted_iota(jnp.int32, (blocks, total), 1)
        column = lax.rem(lax.broadcasted_iota(jnp.int32, (width, total), 1), share)
        spreads = []
        for pattern in range(4):
            high = lax.rem(lane_id // 8, 2) ^ (pattern // 2)
            low = lax.rem(lane_id // 4, 2) ^ (pattern % 2)
            origin = low * devices + lane_id // 16 * 2 + high
            spreads.append(jnp.where(origin == block_id, 1.0, 0.0).astype(BF16))
        for i in range(owned):
            piece = left_wide[pl.ds(i, blocks, stride=owned), :].astype(BF16)
            for pattern in range(4):
                lifted = dot_ta(piece, spreads[pattern])
                chosen = lifted[:width]
                for s in range(1, share):
                    chosen = jnp.where(column == s, lifted[s * width : (s + 1) * width], chosen)
                left_rows[pattern, i * width : (i + 1) * width, :] = chosen.astype(BF16)

    def turn_weight():
        wide_weight[...] = raw_weight_ref[...].astype(F32)
        for k in range(CHUNKS):
            strips = [
                wide_weight[pl.ds(k * per_chunk + e, width, stride=width), :]
                for e in range(per_chunk)
            ]
            columns = slice(k * per_chunk * width, (k + 1) * per_chunk * width)
            weight_ref[:, columns] = jnp.concatenate(strips, axis=0).T.astype(BF16)

    def arrived(k):
        for g in range(GROUPS):
            which = g * CHUNKS + k
            theirs = held_ref.at[pl.ds(which * devices + (1 - core) * rings, rings)]
            remote(theirs, theirs, send_sem, mate_sem.at[which], mate).wait_recv()

    def products(k, quad, col):
        first = slice(quad * 16, quad * 16 + 16)
        cols = slice(col * 256, (col + 1) * 256)
        one, two = (
            held_ref[(g * CHUNKS + k) * devices : (g * CHUNKS + k + 1) * devices, first, cols]
            for g in range(GROUPS)
        )
        row = lax.broadcasted_iota(jnp.int32, one.shape, 1)
        even = lax.rem(row // 4, 2) == 0
        half = devices // 2
        upper = lax.broadcasted_iota(jnp.int32, (half,) + one.shape[1:], 1) < 8
        for low in range(2):
            picked = jnp.where(even, one, two) if low == 0 else jnp.where(even, two, one)
            picked = picked.reshape((half, 2) + one.shape[1:])
            evens, odds = picked[:, 0], picked[:, 1]
            for high in range(2):
                pattern = high * 2 + low
                e = quad * 4 + pattern
                right = jnp.where(upper, evens, odds) if high == 0 else jnp.where(upper, odds, evens)
                product = dot(left_rows[pattern], right.reshape(total, 256)).astype(BF16)
                y_ref[:, e * width : (e + 1) * width, cols] = product.reshape(owned, width, 256)

    def project(k, begin, count):
        columns = slice(k * per_chunk * width, (k + 1) * per_chunk * width)
        for i in range(begin, begin + count):
            part = dot(weight_ref[:, columns], y_ref[i])
            if k > 0:
                part = part + acc_ref[i]
            if k < CHUNKS - 1:
                acc_ref[i] = part
            else:
                pair_ref[i] = part.T * (1.0 / total) + pair_bias_ref[...]

    def pieces(k):
        yield functools.partial(arrived, k)
        for quad in range(per_chunk // 4):
            for col in range(residues // 256):
                yield functools.partial(products, k, quad, col)
        for begin in range(0, owned, 4):
            yield functools.partial(project, k, begin, 4)

    @pl.when(seq == sequences - 1)
    def _():
        pending = []
        last = max(STARTS) + far
        for tick in range(last + 1):
            for k in range(CHUNKS):
                t = tick - STARTS[k]
                if 0 <= t <= far:
                    step(1, k, t)
                    if t == far:
                        pending.extend(pieces(k))
                if tick == 0:
                    step(0, k, far)
            if tick == 0:
                send_left(1)
            if tick == 1:
                turn_weight()
            if tick == far - 2:
                arrange_left()
            for _ in range(5):
                if pending:
                    pending.pop(0)()
        for piece in pending:
            piece()
        sent = left_held.at[pl.ds(0, GROUPS * (devices - 1))]
        remote(sent, sent, left_send_sem, left_recv_sem.at[0], mate).wait_send()
        everything = held_ref.at[pl.ds(0, GROUPS * CHUNKS * (devices - 1))]
        remote(everything, everything, send_sem, mate_sem.at[0], mate).wait_send()


def block(
    devices,
    tokens,
    positions,
    target,
    emb,
    gain_one,
    wq,
    wk,
    wv,
    wg,
    gb,
    wo,
    table,
    gain_two,
    wl,
    wr,
    pair_weight,
    pair_bias,
):
    sequences, residues = tokens.shape
    features = target.shape[1]
    heads = table.shape[1]
    width = wl.shape[1]
    channels = pair_weight.shape[1]
    owned = residues // devices
    rings = devices // 2
    total = devices * sequences
    share = sequences // GROUPS
    operands = (
        tokens,
        positions[None, :],
        target,
        emb,
        gain_one[None, :],
        wq,
        wk,
        wv,
        wg,
        gb[None, :],
        wo,
        table.T,
        gain_two[None, :],
        wl.T,
        wr.T,
        pair_weight,
        pair_bias[None, :],
    )

    def const(a):
        return pl.BlockSpec(
            a.shape, lambda s: (0,) * a.ndim, pipeline_mode=pl.Buffered(buffer_count=1)
        )

    return pl.pallas_call(
        functools.partial(block_kernel, devices, heads),
        grid=(sequences,),
        in_specs=[const(a) for a in operands],
        out_specs=(
            pl.BlockSpec((1, residues, features), lambda s: (s, 0, 0)),
            pl.BlockSpec(memory_space=pltpu.VMEM),
        ),
        out_shape=(
            jax.ShapeDtypeStruct((sequences, residues, features), F32),
            jax.ShapeDtypeStruct((owned, residues, channels), F32),
        ),
        scratch_shapes=[
            pltpu.VMEM((heads, residues, residues), F32),
            pltpu.VMEM((heads, LANES), F32),
            pltpu.VMEM((share, LANES, features), BF16),
            pltpu.VMEM((4, features // LANES, width, LANES), F32),
            pltpu.VMEM((width * width, channels), F32),
            pltpu.VMEM((channels, width * width), BF16),
            pltpu.VMEM((LANES, features), BF16),
            pltpu.VMEM((4, residues, residues), F32),
            pltpu.VMEM((4, residues, residues), BF16),
            pltpu.VMEM((residues, features), F32),
            pltpu.VMEM((GROUPS * residues, LANES), F32),
            pltpu.VMEM((residues // LANES, width * sequences, LANES), F32),
            pltpu.VMEM((GROUPS * devices, owned, LANES), BF16),
            pltpu.VMEM((GROUPS * devices, owned, LANES), BF16),
            pltpu.VMEM((GROUPS * devices * owned, LANES), F32),
            pltpu.VMEM((4, owned * width, total), BF16),
            pltpu.VMEM((GROUPS * CHUNKS * devices, width * share // CHUNKS, residues), BF16),
            pltpu.VMEM((owned, (width // CHUNKS) * width, residues), BF16),
            pltpu.VMEM((owned, channels, residues), F32),
            pltpu.SemaphoreType.DMA,
            pltpu.SemaphoreType.DMA((GROUPS * CHUNKS, rings // 2)),
            pltpu.SemaphoreType.DMA((GROUPS * CHUNKS, rings // 2)),
            pltpu.SemaphoreType.DMA((GROUPS * CHUNKS,)),
            pltpu.SemaphoreType.DMA,
            pltpu.SemaphoreType.DMA((GROUPS,)),
        ],
        compiler_params=pltpu.CompilerParams(
            dimension_semantics=("arbitrary",),
            collective_id=0,
            has_side_effects=True,
            vmem_limit_bytes=60 << 20,
        ),
        cost_estimate=pl.CostEstimate(
            flops=27_000_000_000, bytes_accessed=14 << 20, transcendentals=17_000_000
        ),
        name="msa_block",
    )(*operands)


def shards(
    alignment_token_ids,
    residue_index_offsets,
    target_residue_feature,
    token_embedding_table,
    attention_norm_gain,
    query_weight,
    key_weight,
    value_weight,
    gate_weight,
    gate_offset_bias,
    output_weight,
    relative_position_table,
    product_norm_gain,
    left_weight,
    right_weight,
    pair_weight,
    pair_projection_bias,
):
    return block(
        lax.axis_size("wide"),
        alignment_token_ids,
        residue_index_offsets,
        target_residue_feature,
        token_embedding_table,
        attention_norm_gain,
        query_weight,
        key_weight,
        value_weight,
        gate_weight,
        gate_offset_bias,
        output_weight,
        relative_position_table,
        product_norm_gain,
        left_weight,
        right_weight,
        pair_weight,
        pair_projection_bias,
    )


def solution(mesh):
    placed = (
        P(("groups", "wide"), None),
        P("groups"),
        P("groups", None),
    ) + (P(),) * 14
    return jax.shard_map(
        shards,
        mesh=mesh,
        in_specs=placed,
        out_specs=(P(("groups", "wide"), None, None), P(("groups", "wide"), None, None)),
        check_vma=False,
    )
```

time: 517 us -> 127 us (0.25); the launches traced: 511 us -> 127 us
  matrix products: 201 us -> 0 us
  local copies, waits for them, and re-layouts: 168 us -> 6.67 us
  Pallas kernels: 0 us -> 120 us
  waiting for transfers between devices: 71.6 us -> 0 us
  other arithmetic: 38 us -> 0 us
  starting transfers between devices: 18.6 us -> 0 us
  between operations: 14.3 us -> 0.65 us
    dot_general x59 -> x0, matrix products: 162 us -> none  [the longest x8 54.2 us: row_attention_step(): jnp.einsum('hij,jhd->ihd', weights, value_heads, preferred_element_type=j...]
    convert_element_type x10 -> x0, local copies, waits for them, and re-layouts: 132 us -> none  [the longest x8 131 us: single(): product = product.astype(jnp.bfloat16)]
    pallas_call x0 -> x1, Pallas kernels: none -> 120 us  [block(): pl.pallas_call(functools.partial(block_kernel, devices, heads), grid=(seq...]
    all_gather x1 -> x0, waiting for transfers between devices: 47 us -> none  [shards(): right_whole = lax.all_gather(right, 'wide', axis=0, tiled=True)]
    sub x8 -> x0, matrix products: 39.2 us -> none  [row_attention_step(): scores = scores - jnp.max(scores, axis=-1, keepdims=True)]
    reduce_sum x18 -> x0, other arithmetic: 25.5 us -> none  [the longest x9 13.2 us: layer_normalize(): spread = jnp.mean(centred * centred, axis=-1, keepdims=True)]
    all_to_all x1 -> x0, waiting for transfers between devices: 24.5 us -> none  [shards(): lax.all_to_all(left, 'wide', split_axis=1, concat_axis=0, tiled=True)]
    while x6 -> x0, local copies, waits for them, and re-layouts: 24.4 us -> none
  transfers between devices with their start and end apart: 2 -> 0, of which waited for: 2 -> 0; matrix products, arithmetic and copies ran while one was open for 0% -> 0% of each run, Pallas kernels for 0% -> 0%
where the time goes in v2:
time: 127 us
  Pallas kernels  120 us (94%)
  local copies, waits for them, and re-layouts  6.67 us (5%)
    pallas_call x1, Pallas kernels, block(): pl.pallas_call(functools.partial(block_kernel, devices, heads), grid=(seq...  120 us
    unnamed x4, local copies, waits for them, and re-layouts  6.67 us

profile of v2, /device:TPU:69, one launch (start us, length us, event | category | flops | bytes accessed | tf_op | source)
XLA Modules:
  0.0 127.4 jit_solution(5437601353005305382)
XLA Ops:
  0.6 120.0 %msa_block.1 = (f32[8,512,256]{2,1,0:T(8,128)}, f32[16,512,128]{2,1,0:T(8,128)}) custom-call(s32[8,512]{1,0:T(8,128)} %tok_ref.1, s32[1,512]{1,0:T(1,128)} %bitcast.11, f32[512,256]{1,0:T(8,128)} %target_ref.1, f32[23,256]{1,0:T(8,128)} %emb_ref.1, f32[1,256]{1,0:T(1,128)} %bitcast.12, bf16[256,256]{1,0:T(8,128)(2,1)} %wq_ref.1, bf16[256,256]{1,0:T(8,128)(2,1)} %wk_ref.1, ...), custom_call_target="tpu_custom_call" | custom-call | flops 27000000512 | bytes 14680064 | tf_op jit(solution)/shard_map/msa_block/pallas_call | solution.py:500
  120.7 0.0 copy-start
  120.7 4.7 %copy.21 = f32[8,512,256]{2,1,0:T(8,128)} copy(f32[8,512,256]{2,1,0:T(8,128)} %get-tuple-element.4) | data formatting | bytes 8388608
  125.4 0.0 copy-done
  125.4 2.0 %copy.22 = f32[16,512,128]{2,1,0:T(8,128)} copy(f32[16,512,128]{2,1,0:T(8,128)S(1)} %copy-done) | data formatting | bytes 8388608
Async XLA Ops:
  120.7 4.7 %copy-start = (f32[16,512,128]{2,1,0:T(8,128)S(1)}, f32[16,512,128]{2,1,0:T(8,128)}, u32[]{:S(2)}) copy-start(f32[16,512,128]{2,1,0:T(8,128)} %get-tuple-element.5) | copy-start | bytes 12582916

commit v3 on v2

--- a/solution.py
+++ b/solution.py
@@ -174,17 +174,20 @@
             pl.when(t == 0)(begin)
             pl.when(t > 0)(forward)
 
+    def send_left_to(g, r):
+        target = lax.rem(me + r, devices)
+        remote(
+            left_out.at[g * devices + target],
+            left_held.at[g * devices + mine + place],
+            left_send_sem,
+            left_recv_sem.at[g],
+            target,
+        ).start()
+
     def send_left(g):
         @pl.loop(1, devices)
         def _(r):
-            target = lax.rem(me + r, devices)
-            remote(
-                left_out.at[g * devices + target],
-                left_held.at[g * devices + mine + place],
-                left_send_sem,
-                left_recv_sem.at[g],
-                target,
-            ).start()
+            send_left_to(g, r)
 
     def ring_slot(slot):
         @pl.when(seq >= share)
@@ -193,8 +196,10 @@
             for k in range(CHUNKS):
                 if k // 2 == slot % 2:
                     step(0, k, t)
-            if slot == 0:
-                pl.when(seq == share)(functools.partial(send_left, 0))
+            each = pl.cdiv(devices - 1, 4 * share)
+            first = ((seq - share) * 4 + slot) * each + 1
+            for r in range(each):
+                pl.when(first + r < devices)(functools.partial(send_left_to, 0, first + r))
 
     @pl.when(seq == 0)
     def _():
@@ -287,6 +292,7 @@
             mixed_ref[:, cols] = jnp.where(half_lane == spot, result, mixed_ref[:, cols])
 
     stages = heads // 2
+    slots = {0: 0, 1: 1, stages - 1: 2}
     score(0)
     score(1)
     for stage in range(stages):
@@ -296,7 +302,8 @@
             soften(stage * 2 + which)
             if stage > 0:
                 mix(stage * 2 - 2 + which)
-        ring_slot(stage)
+        if stage in slots:
+            ring_slot(slots[stage])
     mix(heads - 2)
     mix(heads - 1)
 
@@ -304,6 +311,7 @@
     mixed = (mixed_ref[...] * gate).astype(BF16)
     updated = start + dot(mixed, wo_ref[...])
     au_ref[0] = updated
+    ring_slot(3)
     second = layer_normalize(updated, gain_two_ref[...]).astype(BF16)
     group = seq // share
     member = lax.rem(seq, share)

time: 127 us -> 123 us (0.969)
  Pallas kernels: 120 us -> 115 us
    pallas_call x1, Pallas kernels: 120 us -> 115 us  [block(): pl.pallas_call(functools.partial(block_kernel, devices, heads), grid=(seq...]
where the time goes in v3:
time: 123 us
  Pallas kernels  115 us (93%)
  local copies, waits for them, and re-layouts  6.67 us (5%)
    pallas_call x1, Pallas kernels, block(): pl.pallas_call(functools.partial(block_kernel, devices, heads), grid=(seq...  115 us
    unnamed x4, local copies, waits for them, and re-layouts  6.67 us

profile of v3, /device:TPU:69, one launch (start us, length us, event | category | flops | bytes accessed | tf_op | source)
XLA Modules:
  0.0 122.6 jit_solution(1140934240990069113)
XLA Ops:
  0.6 115.3 %msa_block.1 = (f32[8,512,256]{2,1,0:T(8,128)}, f32[16,512,128]{2,1,0:T(8,128)}) custom-call(s32[8,512]{1,0:T(8,128)} %tok_ref.1, s32[1,512]{1,0:T(1,128)} %bitcast.11, f32[512,256]{1,0:T(8,128)} %target_ref.1, f32[23,256]{1,0:T(8,128)} %emb_ref.1, f32[1,256]{1,0:T(1,128)} %bitcast.12, bf16[256,256]{1,0:T(8,128)(2,1)} %wq_ref.1, bf16[256,256]{1,0:T(8,128)(2,1)} %wk_ref.1, ...), custom_call_target="tpu_custom_call" | custom-call | flops 27000000512 | bytes 14680064 | tf_op jit(solution)/shard_map/msa_block/pallas_call | solution.py:508
  115.9 0.0 copy-start
  115.9 4.7 %copy.21 = f32[8,512,256]{2,1,0:T(8,128)} copy(f32[8,512,256]{2,1,0:T(8,128)} %get-tuple-element.4) | data formatting | bytes 8388608
  120.6 0.0 copy-done
  120.6 2.0 %copy.22 = f32[16,512,128]{2,1,0:T(8,128)} copy(f32[16,512,128]{2,1,0:T(8,128)S(1)} %copy-done) | data formatting | bytes 8388608
Async XLA Ops:
  115.9 4.7 %copy-start = (f32[16,512,128]{2,1,0:T(8,128)S(1)}, f32[16,512,128]{2,1,0:T(8,128)}, u32[]{:S(2)}) copy-start(f32[16,512,128]{2,1,0:T(8,128)} %get-tuple-element.5) | copy-start | bytes 12582916
